TPU v7x, 32 devices: a whole 2x2x4 slice. The times are simulated.
32 devices in a mesh: replica: 2 (over x), data: 4 (over z), table: 4 (over y, core).
Axes of the slice: x: 2, y: 2, z: 4, core: 2. Of those that a mesh axis runs over, the one named last changes fastest.
Arguments:
- tokens: bfloat16 [2048, 768], P(('replica', 'data', 'table')), parts along dimension 0
- grad_out: bfloat16 [2048, 768], P(('replica', 'data', 'table')), parts along dimension 0
- table_u: bfloat16 [131072, 768], P(('replica', 'table')), parts along dimension 0
- table_v: bfloat16 [131072, 768], P(('replica', 'table')), parts along dimension 0
- wanted_ids: int32 [32, 128], P(('replica', 'data', 'table')), parts along dimension 0
- pick_idx: int32 [2048, 4, 32], P(('replica', 'data', 'table')), parts along dimension 0
- gate_val: float32 [2048, 4, 32], P(('replica', 'data', 'table')), parts along dimension 0
Outputs:
- output 1: bfloat16 [2048, 768], P(('replica', 'data', 'table')), parts along dimension 0
- output 2: bfloat16 [2048, 768], P(('replica', 'data', 'table')), parts along dimension 0
- output 3: bfloat16 [131072, 768], P(('replica', 'table')), parts along dimension 0
- output 4: bfloat16 [131072, 768], P(('replica', 'table')), parts along dimension 0
There are 2 independent parts. A program takes and returns all parts, laid end to end along the dimension named above; each array names one.
All inputs are finite; a program needn't handle non-finite values.
Results may differ from a plain program's by a relative error of at most 0.00789345.
Values are sent between devices in bfloat16 or wider.
A program may use at most 1 GiB of HBM per device.

v0:
```python
import functools

import jax
import jax.numpy as jnp
from jax import lax
from jax.experimental import pallas as pl
from jax.experimental.pallas import tpu as pltpu
from jax.sharding import PartitionSpec as P

MESH = pl.DeviceIdType.MESH
F32 = jnp.float32
BF16 = jnp.bfloat16
VMEM = pl.BlockSpec(memory_space=pltpu.VMEM)
ANY = pl.BlockSpec(memory_space=pl.ANY)
NT = (((1,), (1,)), ((), ()))
TN = (((0,), (0,)), ((), ()))
HBM = pl.BlockSpec(memory_space=pltpu.HBM)
SMEM = pl.BlockSpec(memory_space=pltpu.SMEM)
MB = 1024 * 1024
UP, DOWN, YY, CC = range(4)


def gelu_pair(pre_act):
    cdf_val = 0.5 * (1.0 + lax.erf(pre_act * 0.7071067811865476))
    pdf_val = jnp.exp(-0.5 * pre_act * pre_act) * 0.3989422804014327
    return pre_act * cdf_val, cdf_val + pre_act * pdf_val


def split3(val):
    one = val.astype(BF16)
    rest = val - one.astype(F32)
    two = rest.astype(BF16)
    three = (rest - two.astype(F32)).astype(BF16)
    return one, two, three


def dot(a, b, dims=None):
    if dims is None:
        return jnp.dot(a, b, preferred_element_type=F32)
    return lax.dot_general(a, b, dims, preferred_element_type=F32)


def first_kernel(ids_ref, x_ref, dy_ref, ids_out, xd, dyd, xu, dyu, xy, dyy, ssem, rsem, hops, hopr):
    z = lax.axis_index("data")
    t = lax.axis_index("table")
    me = z * 4 + t
    bar = pltpu.get_barrier_semaphore()
    peers = [(lax.rem(z + dz, 4), lax.rem(t + dt, 4)) for dz in range(4) for dt in range(4)][1:]
    for pz, pt in peers:
        pl.semaphore_signal(bar, inc=1, device_id={"data": pz, "table": pt}, device_id_type=MESH)
    pl.semaphore_wait(bar, 15)
    copies = []
    for i, (pz, pt) in enumerate(peers):
        copies.append(pltpu.make_async_remote_copy(
            src_ref=ids_ref, dst_ref=ids_out.at[me], send_sem=ssem.at[i], recv_sem=rsem.at[i],
            device_id={"data": pz, "table": pt}, device_id_type=MESH,
        ))
        copies[-1].start()

    def hop(k, lane):
        dst = ((xd, dyd), (xu, dyu), (xy, dyy))[lane][k]
        peer = ({"data": z + 1}, {"data": z - 1}, {"table": lax.rem(t + 2, 4)})[lane]
        return pltpu.make_async_remote_copy(
            src_ref=(x_ref, dy_ref)[k], dst_ref=dst, send_sem=hops.at[k, lane], recv_sem=hopr.at[k, lane],
            device_id=peer, device_id_type=MESH,
        )

    for k in range(2):
        hop(k, 2).start()

        @pl.when(z < 3)
        def _():
            hop(k, 0).start()

        @pl.when(z > 0)
        def _():
            hop(k, 1).start()

    local = pltpu.make_async_copy(ids_ref, ids_out.at[me], ssem.at[15])
    local.start()
    local.wait()
    for one in copies:
        one.wait()
    for k in range(2):
        hop(k, 2).wait()

        @pl.when(z < 3)
        def _():
            hop(k, 0).wait_send()
            hop(k, 1).wait_recv()

        @pl.when(z > 0)
        def _():
            hop(k, 1).wait_send()
            hop(k, 0).wait_recv()


def prep_kernel(u_hbm, v_hbm, pick_hbm, gate_hbm, ids_ref, du_hbm, g_out, rows_u, rows_v, vslot, meta,
                zbuf, ugrp, vgrp, uacc, vacc, pick_ref, gate_ref, sslot, zsem, gsem, ssem, isem):
    r = lax.axis_index("table")
    n_local = u_hbm.shape[0]
    n_ent = rows_u.shape[0]
    zrows = zbuf.shape[0]
    load_pick = pltpu.make_async_copy(pick_hbm, pick_ref, isem.at[0])
    load_gate = pltpu.make_async_copy(gate_hbm, gate_ref, isem.at[1])
    load_pick.start()
    load_gate.start()
    zbuf[...] = jnp.zeros_like(zbuf)

    ids = jnp.concatenate([ids_ref[e] for e in range(16)], axis=0).astype(F32)
    pick = ids[:, 0:32]
    for o in range(1, 4):
        pick = jnp.where(r == o, ids[:, o * 32 : o * 32 + 32], pick)
    pick = pick - (r * n_local).astype(F32)
    idrow = jnp.concatenate([pick[e : e + 1, :] for e in range(16)], axis=1)
    ii = lax.broadcasted_iota(jnp.int32, (n_ent, n_ent), 0)
    jj = lax.broadcasted_iota(jnp.int32, (n_ent, n_ent), 1)

    def fill(i):
        return pltpu.make_async_copy(zbuf, du_hbm.at[pl.ds(i * zrows, zrows), :], zsem)

    for i in range(n_local // zrows):
        fill(i).start()

    def lanes(cond, val):
        return jnp.sum(jnp.where(cond, val, 0.0), axis=1, keepdims=True)

    def subl(cond, val):
        return jnp.sum(jnp.where(cond, val, 0.0), axis=0, keepdims=True)

    idcol = lanes(ii == jj, jnp.broadcast_to(idrow, (n_ent, n_ent)))
    grow, gcol = jnp.floor(idrow * 0.125), jnp.floor(idcol * 0.125)
    same = gcol == grow
    lead_col = jnp.where(lanes(same & (jj < ii), 1.0) == 0.0, 1.0, 0.0)
    lead_row = jnp.where(subl(same & (ii < jj), 1.0) == 0.0, 1.0, 0.0)
    rank_col = lanes(jj < ii, jnp.broadcast_to(lead_row, (n_ent, n_ent)))
    rank_row = subl(ii < jj, jnp.broadcast_to(lead_col, (n_ent, n_ent)))
    hit_c = (rank_col.astype(jnp.int32) == jj) & (lead_col > 0.0)
    hit_r = (rank_row.astype(jnp.int32) == ii) & (lead_row > 0.0)
    icount = jnp.sum(lead_row, axis=1, keepdims=True).astype(jnp.int32)
    slot_row = subl(hit_c, jnp.broadcast_to(gcol, (n_ent, n_ent)))
    slot_col = lanes(hit_r, jnp.broadcast_to(grow, (n_ent, n_ent)))
    vslot[0:1, :] = slot_row.astype(jnp.int32)
    vslot[1:8, :] = jnp.broadcast_to(icount, (7, n_ent))
    slot_row = jnp.where(jj[0:1, :] < icount, slot_row, -1.0)
    slot_col = jnp.where(ii[:, 0:1] < icount, slot_col, -1.0)
    meta[0:1, :] = idrow
    meta[1:8, :] = jnp.broadcast_to(slot_row, (7, n_ent))

    to_smem = pltpu.make_async_copy(vslot, sslot, ssem)
    to_smem.start()
    to_smem.wait()
    n_blk = (sslot[1, 0] + 31) // 32

    def fetch(k, table, grp, s):
        g = pl.multiple_of(sslot[0, k] * 8, 8)
        return pltpu.make_async_copy(table.at[pl.ds(g, 8), :], grp.at[pl.ds(pl.multiple_of(k * 8, 8), 8), :], gsem.at[s])

    def start_fetch(k, carry):
        fetch(k, u_hbm, ugrp, 0).start()
        fetch(k, v_hbm, vgrp, 1).start()
        return carry

    def wait_fetch(k, carry):
        fetch(k, u_hbm, ugrp, 0).wait()
        fetch(k, v_hbm, vgrp, 1).wait()
        return carry

    lax.fori_loop(0, n_blk * 32, start_fetch, 0)

    load_pick.wait()
    load_gate.wait()
    sel, tok = pick_ref.shape
    quarter = sel // 4
    row = lax.broadcasted_iota(jnp.int32, (2 * quarter, 2 * tok), 0)
    row = row + jnp.where(row >= quarter, quarter, 0)

    def add_gates(i, acc):
        base = pl.multiple_of(i * 8, 8)
        pick8 = pick_ref[pl.ds(base, 8), :]
        gate8 = gate_ref[pl.ds(base, 8), :]
        pick8 = jnp.concatenate([pick8, pick8 - quarter], axis=1)
        gate8 = jnp.concatenate([gate8, gate8], axis=1)
        for j in range(8):
            acc = acc + jnp.where(row == pick8[j : j + 1, :], gate8[j : j + 1, :], 0.0)
        return acc

    g_out[...] = lax.fori_loop(0, sel // 8, add_gates, jnp.zeros((2 * quarter, 2 * tok), F32))

    lax.fori_loop(0, n_blk * 32, wait_fetch, 0)

    uacc[...] = jnp.zeros_like(uacc)
    vacc[...] = jnp.zeros_like(vacc)
    kk = lax.broadcasted_iota(jnp.int32, (n_ent, 256), 0)
    qk = lax.broadcasted_iota(jnp.int32, (n_ent, 256), 1) >> 3
    q7 = (lax.broadcasted_iota(jnp.int32, (1, 256), 1) & 7).astype(F32)

    def take_rows(b, carry):
        rowid = 8.0 * subl(kk == qk + b * 32, jnp.broadcast_to(slot_col, (n_ent, 256))) + q7
        pickm = jnp.where(idcol == rowid, 1.0, 0.0).astype(BF16)
        base = pl.multiple_of(b * 256, 256)
        uacc[...] += dot(pickm, ugrp[pl.ds(base, 256), :])
        vacc[...] += dot(pickm, vgrp[pl.ds(base, 256), :])
        return carry

    lax.fori_loop(0, n_blk, take_rows, 0)
    rows_u[...] = uacc[...].astype(BF16)
    rows_v[...] = vacc[...].astype(BF16)
    for i in range(n_local // zrows):
        fill(i).wait()


def main_kernel(x_ref, dy_ref, g_ref, xd, dyd, xu, dyu, xy, dyy, ru, rv, pu, pv, y_out, dx_out,
                tx, ty, gx, ubuf, vbuf, ssem, rsem, rows_s, rows_r):
    z = lax.axis_index("data")
    t = lax.axis_index("table")
    y, c = t // 2, lax.rem(t, 2)
    t_y = (1 - y) * 2 + c
    t_c = y * 2 + (1 - c)
    t_yc = (1 - y) * 2 + (1 - c)
    y_peer, c_peer = {"table": t_y}, {"table": t_c}
    up, down = {"data": z + 1}, {"data": z - 1}
    peers = {UP: up, DOWN: down, YY: y_peer, CC: c_peer}
    tok = x_ref.shape[0]
    low_at = {d: z - d >= 0 for d in (1, 2, 3)}
    high_at = {d: z + d <= 3 for d in (1, 2, 3)}
    can_up, can_down = high_at[1], low_at[1]
    middle = can_up & can_down
    ends = (z == 0) | (z == 3)

    bar = pltpu.get_barrier_semaphore()
    for peer in (t_y, t_c, t_yc):
        pl.semaphore_signal(bar, inc=1, device_id={"table": peer}, device_id_type=MESH)

    @pl.when(can_up)
    def _():
        pl.semaphore_signal(bar, inc=1, device_id=up, device_id_type=MESH)

    @pl.when(can_down)
    def _():
        pl.semaphore_signal(bar, inc=1, device_id=down, device_id_type=MESH)

    pl.semaphore_wait(bar, 3 + can_up.astype(jnp.int32) + can_down.astype(jnp.int32))

    outs = (gx, tx, ty)
    TOKS = (1, 2)
    sent = []

    def place(k, slot):
        if k == 0:
            return gx.at[slot]
        return outs[k].at[pl.ds(pl.multiple_of(slot * tok, tok), tok), :]

    def copy(k, slot, lane, src=None):
        ref = place(k, slot)
        return pltpu.make_async_remote_copy(
            src_ref=ref if src is None else src, dst_ref=ref,
            send_sem=ssem.at[k, lane, slot], recv_sem=rsem.at[k, slot],
            device_id=peers[lane], device_id_type=MESH,
        )

    def when(cond, run):
        if cond is None:
            run()
        else:
            @pl.when(cond)
            def _():
                run()

    def start(cond, k, slot, lane, src=None):
        sent.append((cond, k, slot, lane))
        when(cond, lambda: copy(k, slot, lane, src).start())

    def arrive(cond, k, slot):
        when(cond, lambda: copy(k, slot, CC).wait_recv())

    def zs(d):
        return (z + d) * 4 + t

    def ys(d):
        return (z + d) * 4 + t_y

    def send_row(k, s):
        to = lax.rem(t + s, 4)
        return pltpu.make_async_remote_copy(
            src_ref=(ru, rv)[k].at[pl.ds(pl.multiple_of(z * 128 + to * 32, 32), 32), :],
            dst_ref=(ubuf, vbuf)[k].at[pl.ds(pl.multiple_of(t * 32, 32), 32), :],
            send_sem=rows_s.at[k, s], recv_sem=rows_r.at[k, s],
            device_id={"table": to}, device_id_type=MESH,
        )

    own = (None, x_ref, dy_ref)
    low = (None, xd, dyd)
    high = (None, xu, dyu)
    across = (None, xy, dyy)
    me = zs(0)
    my_half = g_ref.at[pl.ds(pl.multiple_of(y * 32, 32), 32), :]
    other_half = g_ref.at[pl.ds(pl.multiple_of((1 - y) * 32, 32), 32), :]

    start(can_up, 0, me, UP, my_half)
    start(can_down, 0, me, DOWN, my_half)
    start(None, 0, me, YY, other_half)
    start(None, 0, me, CC, my_half)
    for k in TOKS:
        start(middle, k, zs(-1), UP, low[k])
        start(middle, k, zs(1), DOWN, high[k])
    for k in range(2):
        for s in (2, 1, 3):
            send_row(k, s).start()
    for k in TOKS:
        start(z < 2, k, ys(0), UP, across[k])
        start(z > 1, k, ys(0), DOWN, across[k])
        start(None, k, me, CC, own[k])
        start(None, k, ys(0), CC, across[k])
        start(can_down, k, zs(-1), CC, low[k])
        start(can_up, k, zs(1), CC, high[k])

    def keep(cond, k, slot, src):
        def run():
            outs[k][pl.ds(pl.multiple_of(slot * tok, tok), tok), :] = src[...]

        when(cond, run)

    gx[me] = g_ref[pl.ds(pl.multiple_of(y * 32, 32), 32), :]
    for k in TOKS:
        keep(None, k, me, own[k])
        keep(None, k, ys(0), across[k])
        keep(can_down, k, zs(-1), low[k])
        keep(can_up, k, zs(1), high[k])
    mine = pl.ds(pl.multiple_of(t * 32, 32), 32)
    ubuf[mine, :] = ru[pl.ds(pl.multiple_of(z * 128 + t * 32, 32), 32), :]
    vbuf[mine, :] = rv[pl.ds(pl.multiple_of(z * 128 + t * 32, 32), 32), :]

    def gates_on(slot_of, d):
        arrive(low_at[d], 0, slot_of(-d))
        start(low_at[d] & can_up, 0, slot_of(-d), UP)
        start(low_at[d], 0, slot_of(-d), CC)
        arrive(high_at[d], 0, slot_of(d))
        start(high_at[d] & can_down, 0, slot_of(d), DOWN)
        start(high_at[d], 0, slot_of(d), CC)

    def tokens_on(d):
        for k in TOKS:
            arrive(low_at[d], k, zs(-d))
            start(low_at[d] & can_up, k, zs(-d), UP)
            start(low_at[d], k, zs(-d), YY)
            arrive(high_at[d], k, zs(d))
            start(high_at[d] & can_down, k, zs(d), DOWN)
            start(high_at[d], k, zs(d), YY)
            start(low_at[d], k, zs(-d), CC)
            start(high_at[d], k, zs(d), CC)

    def crossed(cond, d):
        for k in TOKS:
            arrive(cond, k, ys(d))
            start(cond, k, ys(d), CC)

    diag = (lax.broadcasted_iota(jnp.int32, (128, 256), 0) >> 5) == (lax.broadcasted_iota(jnp.int32, (128, 256), 1) >> 6)

    def products(d):
        for tt in (t_c, t_yc):
            for k in range(3):
                arrive(None, k, d * 4 + tt)
        tsl = pl.ds(pl.multiple_of(d * 256, 256), 256)
        esl = pl.ds(pl.multiple_of(d * 128, 128), 128)
        x4, dy4 = tx[tsl, :], ty[tsl, :]
        u4, v4 = ru[esl, :], rv[esl, :]
        gates = []
        for e in range(4):
            part = gx[d * 4 + e]
            part = jnp.where(c == 1, part[:, 64:128], part[:, 0:64])
            gates.append(jnp.concatenate([part] * 4, axis=1))
        g4 = jnp.concatenate(gates, axis=0)
        act, slope = gelu_pair(dot(u4, x4, NT))
        b4 = dot(v4, dy4, NT)
        w4 = jnp.where(diag, g4 * act, 0.0)
        c4 = jnp.where(diag, g4 * slope * b4, 0.0)
        for coef, val, out in ((c4, x4, pu), (w4, dy4, pv)):
            full = dot(jnp.concatenate(split3(coef), axis=0), val)
            full = full[0:128] + full[128:256] + full[256:384]
            for k, term in enumerate(split3(full)):
                out[k, esl, :] = term

    gates_on(zs, 1)
    arrive(None, 0, ys(0))
    start(can_up, 0, ys(0), UP)
    start(can_down, 0, ys(0), DOWN)
    start(None, 0, ys(0), CC)
    gates_on(zs, 2)
    gates_on(ys, 1)
    products(z)
    tokens_on(2)
    for k in TOKS:
        start(z == 2, k, ys(0), UP, across[k])
        start(z == 1, k, ys(0), DOWN, across[k])
    gates_on(zs, 3)
    gates_on(ys, 2)
    gates_on(ys, 3)

    gates = jnp.concatenate([g_ref[0:32, 0:64], g_ref[0:32, 64:128], g_ref[32:64, 0:64], g_ref[32:64, 64:128]], axis=0)
    for s in range(1, 4):
        send_row(0, s).wait_recv()
        send_row(1, s).wait_recv()
    act, slope = gelu_pair(dot(ubuf[...], x_ref[...], NT))
    b_val = dot(vbuf[...], dy_ref[...], NT)
    w_val = jnp.transpose(gates * act)
    c_val = jnp.transpose(gates * slope * b_val)
    for coef, rows, out in ((w_val, vbuf, y_out), (c_val, ubuf, dx_out)):
        full = dot(jnp.concatenate(split3(coef), axis=0), rows[...])
        out[...] = (full[0:64] + full[64:128] + full[128:192]).astype(BF16)

    tokens_on(3)
    crossed(middle, -1)
    crossed(middle, 1)
    when(middle, lambda: products(z - 1))
    when(middle, lambda: products(z + 1))
    crossed(low_at[2], -2)
    crossed(high_at[2], 2)
    products(lax.rem(z + 2, 4))
    crossed(z == 3, -1)
    crossed(z == 0, 1)
    when(ends, lambda: products(1 + z // 3))
    crossed(low_at[3], -3)
    crossed(high_at[3], 3)
    when(ends, lambda: products(3 - z))

    for k in range(2):
        for s in range(1, 4):
            send_row(k, s).wait_send()
    for cond, k, slot, lane in sent:
        when(cond, lambda k=k, slot=slot, lane=lane: copy(k, slot, lane).wait_send())


def put_kernel(pu, pv, y_ref, dx_ref, sslot, meta, du_in, du_hbm, dv_hbm, y_out, dx_out, zbuf, ures, vres, zsem, psem):
    n_ent = pu.shape[1]
    zrows = zbuf.shape[0]
    zbuf[...] = jnp.zeros_like(zbuf)
    y_out[...] = y_ref[...]
    dx_out[...] = dx_ref[...]
    n_slot = sslot[1, 0]
    n_blk = (n_slot + 31) // 32
    idrow, slot_row = meta[0:1, :], meta[1:2, :]
    kq = lax.broadcasted_iota(jnp.int32, (256, n_ent), 1)
    qq = lax.broadcasted_iota(jnp.int32, (256, n_ent), 0) >> 3
    q7 = (lax.broadcasted_iota(jnp.int32, (256, 1), 0) & 7).astype(F32)

    def fill(i):
        return pltpu.make_async_copy(zbuf, dv_hbm.at[pl.ds(i * zrows, zrows), :], zsem)

    for i in range(dv_hbm.shape[0] // zrows):
        fill(i).start()

    def patch(k, table, res, s):
        g = pl.multiple_of(sslot[0, k] * 8, 8)
        return pltpu.make_async_copy(res.at[pl.ds(pl.multiple_of(k * 8, 8), 8), :], table.at[pl.ds(g, 8), :], psem.at[s])

    def put_rows(b, carry):
        rowid = 8.0 * jnp.sum(jnp.where(kq == qq + b * 32, slot_row, 0.0), axis=1, keepdims=True) + q7
        spread = jnp.where(rowid == idrow, 1.0, 0.0).astype(BF16)
        base = pl.multiple_of(b * 256, 256)
        ures[pl.ds(base, 256), :] = (dot(spread, pu[0]) + dot(spread, pu[1]) + dot(spread, pu[2])).astype(BF16)
        vres[pl.ds(base, 256), :] = (dot(spread, pv[0]) + dot(spread, pv[1]) + dot(spread, pv[2])).astype(BF16)
        return carry

    lax.fori_loop(0, n_blk, put_rows, 0)

    def over_slots(run):
        def body(k, carry):
            run(k)
            return carry

        lax.fori_loop(0, n_slot, body, 0)

    over_slots(lambda k: patch(k, du_hbm, ures, 0).start())
    for i in range(dv_hbm.shape[0] // zrows):
        fill(i).wait()
    over_slots(lambda k: patch(k, dv_hbm, vres, 1).start())
    over_slots(lambda k: patch(k, du_hbm, ures, 0).wait())
    over_slots(lambda k: patch(k, dv_hbm, vres, 1).wait())


def solution(mesh):
    tok_spec = P(('replica', 'data', 'table'))
    row_spec = P(('replica', 'table'))

    def device_step(tok, dy, u, v, wanted, pick, gate):
        n_tok, width = tok.shape
        n_local = u.shape[0]
        sel = pick.shape[1] * pick.shape[2]
        shape = jax.ShapeDtypeStruct
        dma = pltpu.SemaphoreType.DMA
        rows = shape((512, width), BF16)
        block = shape((n_tok, width), BF16)
        table = shape((n_local, width), BF16)
        pick_t = jnp.transpose(pick, (1, 2, 0)).reshape(sel, n_tok)
        gate_t = jnp.transpose(gate, (1, 2, 0)).reshape(sel, n_tok)

        ids, *hops = pl.pallas_call(
            first_kernel, out_shape=[shape((16, 1, 128), jnp.int32)] + [block] * 6,
            in_specs=[HBM] * 3, out_specs=[VMEM] * 7,
            scratch_shapes=[dma((16,)), dma((15,)), dma((2, 3)), dma((2, 3))],
            compiler_params=pltpu.CompilerParams(collective_id=0, has_side_effects=True, vmem_limit_bytes=4 * MB),
        )(wanted, tok, dy)
        du, g_own, ru, rv, vslot, meta = pl.pallas_call(
            prep_kernel,
            out_shape=[table, shape((64, 128), F32), rows, rows, shape((8, 512), jnp.int32), shape((8, 512), F32)],
            in_specs=[HBM] * 4 + [VMEM], out_specs=[HBM] + [VMEM] * 5,
            scratch_shapes=[
                pltpu.VMEM((512, width), BF16), pltpu.VMEM((4096, width), BF16), pltpu.VMEM((4096, width), BF16),
                pltpu.VMEM((512, width), F32), pltpu.VMEM((512, width), F32),
                pltpu.VMEM((sel, n_tok), jnp.int32), pltpu.VMEM((sel, n_tok), F32),
                pltpu.SMEM((8, 512), jnp.int32), dma, dma((2,)), dma, dma((2,)),
            ],
            compiler_params=pltpu.CompilerParams(vmem_limit_bytes=36 * MB),
        )(u, v, pick_t, gate_t, ids)
        pu, pv, y, dx = pl.pallas_call(
            main_kernel,
            out_shape=[shape((3, 512, width), BF16)] * 2 + [block] * 2,
            in_specs=[VMEM] * 11, out_specs=[VMEM] * 4,
            scratch_shapes=[
                pltpu.VMEM((16 * n_tok, width), BF16), pltpu.VMEM((16 * n_tok, width), BF16),
                pltpu.VMEM((16, 32, 128), F32), pltpu.VMEM((128, width), BF16), pltpu.VMEM((128, width), BF16),
                dma((3, 4, 16)), dma((3, 16)), dma((2, 4)), dma((2, 4)),
            ],
            compiler_params=pltpu.CompilerParams(collective_id=1, has_side_effects=True, vmem_limit_bytes=32 * MB),
        )(tok, dy, g_own, *hops, ru, rv)
        du, dv, y, dx = pl.pallas_call(
            put_kernel,
            out_shape=[table, table, block, block],
            in_specs=[VMEM] * 4 + [SMEM, VMEM, HBM], out_specs=[HBM, HBM, VMEM, VMEM],
            scratch_shapes=[
                pltpu.VMEM((512, width), BF16), pltpu.VMEM((4096, width), BF16), pltpu.VMEM((4096, width), BF16),
                dma, dma((2,)),
            ],
            input_output_aliases={6: 0},
            compiler_params=pltpu.CompilerParams(vmem_limit_bytes=36 * MB),
        )(pu, pv, y, dx, vslot, meta, du)
        return y, dx, du, dv

    return jax.shard_map(device_step, mesh=mesh, in_specs=(tok_spec, tok_spec, row_spec, row_spec, tok_spec, tok_spec, tok_spec), out_specs=(tok_spec, tok_spec, row_spec, row_spec), check_vma=False)
```

profile of v0, /device:TPU:0, one launch (start us, length us, event | category | flops | bytes accessed | tf_op | source)
XLA Modules:
  0.0 72.3 jit_solution(11233906018275937552)
XLA Ops:
  0.6 0.0 copy-start
  0.6 0.9 %copy-done = bf16[64,768]{1,0:T(8,128)(2,1)S(1)} copy-done((bf16[64,768]{1,0:T(8,128)(2,1)S(1)}, bf16[64,768]{1,0:T(8,128)(2,1)}, u32[]{:S(2)}) %copy-start) | copy-done | bytes 98328
  1.5 0.0 copy-start.2
  1.5 0.9 %copy-done.2 = bf16[64,768]{1,0:T(8,128)(2,1)S(1)} copy-done((bf16[64,768]{1,0:T(8,128)(2,1)S(1)}, bf16[64,768]{1,0:T(8,128)(2,1)}, u32[]{:S(2)}) %copy-start.2) | copy-done | bytes 98328
  2.4 0.0 copy-start.6
  2.4 0.7 copy-done.6
  3.1 12.5 %shard_map.102 = (s32[16,1,128]{2,1,0:T(1,128)S(1)}, bf16[64,768]{1,0:T(8,128)(2,1)S(1)}, bf16[64,768]{1,0:T(8,128)(2,1)S(1)}, bf16[64,768]{1,0:T(8,128)(2,1)S(1...) custom-call(s32[1,128]{1,0:T(1,128)S(1)} %copy-done.6, ...), custom_call_target="tpu_custom_call" | custom-call | tf_op jit(solution)/shard_map/pallas_call | solution.py:498
  15.6 0.0 copy-start.4
  15.6 0.8 %copy-done.4 = s32[64,4,32]{0,2,1:T(8,128)S(1)} copy-done((s32[64,4,32]{0,2,1:T(8,128)S(1)}, s32[64,4,32]{0,2,1:T(8,128)}, u32[]{:S(2)}) %copy-start.4) | copy-done | bytes 32792
  16.5 0.0 copy-start.5
  16.5 0.8 %copy-done.5 = f32[64,4,32]{0,2,1:T(8,128)S(1)} copy-done((f32[64,4,32]{0,2,1:T(8,128)S(1)}, f32[64,4,32]{0,2,1:T(8,128)}, u32[]{:S(2)}) %copy-start.5) | copy-done | bytes 32792
  17.3 0.0 copy-start.1
  17.3 0.0 copy-start.3
  17.3 10.0 %shard_map.103 = (bf16[16384,768]{1,0:T(8,128)(2,1)}, f32[64,128]{1,0:T(8,128)S(1)}, bf16[512,768]{1,0:T(8,128)(2,1)S(1)}, bf16[512,768]{1,0:T(8,128)(2,1)S(1)},...) custom-call(bf16[16384,768]{1,0:T(8,128)(2,1)} %u_hbm.1, bf16[16384,768]{1,0:T(8,128)(2,1)} %v_hbm.1, s32[128,64]{1,0:T(8,128)S(1)} %bitcast.6, ...), custom_call_target="tpu_custom_call" | custom-call | tf_op jit(solution)/shard_map/pallas_call | solution.py:504
  27.3 0.0 copy-done.1
  27.3 0.0 copy-done.3
  27.3 33.6 %shard_map.104 = (bf16[3,512,768]{2,1,0:T(8,128)(2,1)S(1)}, bf16[3,512,768]{2,1,0:T(8,128)(2,1)S(1)}, bf16[64,768]{1,0:T(8,128)(2,1)S(1)}, bf16[64,768]{1,0:T(8,128)(2,1)S(1)}) custom-call(bf16[64,768]{1,0:T(8,128)(2,1)S(1)} %copy-done.1, bf16[64,768]{1,0:T(8,128)(2,1)S(1)} %copy-done.3, f32[64,128]{1,0:T(8,128)S(1)} %get-tuple-element.26.g_ref, ...), custom_call_target="tpu_custom_call" | custom-call | tf_op jit(solution)/shard_map/pallas_call | solution.py:516
  60.9 11.4 %shard_map.105 = (bf16[16384,768]{1,0:T(8,128)(2,1)}, bf16[16384,768]{1,0:T(8,128)(2,1)}, bf16[64,768]{1,0:T(8,128)(2,1)}, bf16[64,768]{1,0:T(8,128)(2,1)}) custom-call(bf16[3,512,768]{2,1,0:T(8,128)(2,1)S(1)} %get-tuple-element.35.pu, bf16[3,512,768]{2,1,0:T(8,128)(2,1)S(1)} %get-tuple-element.36.pv, ...), custom_call_target="tpu_custom_call", output_to_operand_aliasing={{0}: (6, {})} | custom-call | tf_op jit(solution)/shard_map/pallas_call | solution.py:527
Async XLA Ops:
  0.6 0.9 %copy-start = (bf16[64,768]{1,0:T(8,128)(2,1)S(1)}, bf16[64,768]{1,0:T(8,128)(2,1)}, u32[]{:S(2)}) copy-start(bf16[64,768]{1,0:T(8,128)(2,1)} %x_ref.3) | copy-start | bytes 294916
  1.5 0.9 %copy-start.2 = (bf16[64,768]{1,0:T(8,128)(2,1)S(1)}, bf16[64,768]{1,0:T(8,128)(2,1)}, u32[]{:S(2)}) copy-start(bf16[64,768]{1,0:T(8,128)(2,1)} %dy_ref.3) | copy-start | bytes 294916
  2.4 0.7 copy-start.6
  15.6 0.8 %copy-start.4 = (s32[64,4,32]{0,2,1:T(8,128)S(1)}, s32[64,4,32]{0,2,1:T(8,128)}, u32[]{:S(2)}) copy-start(s32[64,4,32]{0,2,1:T(8,128)} %param.12) | copy-start | bytes 98308
  16.5 0.8 %copy-start.5 = (f32[64,4,32]{0,2,1:T(8,128)S(1)}, f32[64,4,32]{0,2,1:T(8,128)}, u32[]{:S(2)}) copy-start(f32[64,4,32]{0,2,1:T(8,128)} %param.13) | copy-start | bytes 98308
  17.3 10.0 %copy-start.1 = (bf16[64,768]{1,0:T(8,128)(2,1)S(1)}, bf16[64,768]{1,0:T(8,128)(2,1)}, u32[]{:S(2)}) copy-start(bf16[64,768]{1,0:T(8,128)(2,1)} %x_ref.3) | copy-start | bytes 294916
  17.3 10.0 %copy-start.3 = (bf16[64,768]{1,0:T(8,128)(2,1)S(1)}, bf16[64,768]{1,0:T(8,128)(2,1)}, u32[]{:S(2)}) copy-start(bf16[64,768]{1,0:T(8,128)(2,1)} %dy_ref.3) | copy-start | bytes 294916
where the time goes:
time: 73.5 us; the launch traced here: 72.3 us
  Pallas kernels  67.5 us (92%)
  local copies, waits for them, and re-layouts  4.12 us (6%)
    pallas_call x1, Pallas kernels, device_step(): pl.pallas_call(main_kernel, out_shape=[shape((3, 512, width), BF16)] * 2...  33.6 us
    pallas_call x1, Pallas kernels, device_step(): pl.pallas_call(first_kernel, out_shape=[shape((16, 1, 128), jnp.int32)] +...  12.5 us
    pallas_call x1, Pallas kernels, device_step(): pl.pallas_call(put_kernel, out_shape=[table, table, block, block], in_spe...  11.4 us
    pallas_call x1, Pallas kernels, device_step(): pl.pallas_call(prep_kernel, out_shape=[table, shape((64, 128), F32), rows...  9.95 us
    unnamed x14, local copies, waits for them, and re-layouts  4.12 us

commit v1 on v0

--- a/solution.py
+++ b/solution.py
@@ -308,8 +308,6 @@
         for s in (2, 1, 3):
             send_row(k, s).start()
     for k in TOKS:
-        start(z < 2, k, ys(0), UP, across[k])
-        start(z > 1, k, ys(0), DOWN, across[k])
         start(None, k, me, CC, own[k])
         start(None, k, ys(0), CC, across[k])
         start(can_down, k, zs(-1), CC, low[k])
@@ -331,13 +329,15 @@
     ubuf[mine, :] = ru[pl.ds(pl.multiple_of(z * 128 + t * 32, 32), 32), :]
     vbuf[mine, :] = rv[pl.ds(pl.multiple_of(z * 128 + t * 32, 32), 32), :]
 
-    def gates_on(slot_of, d):
-        arrive(low_at[d], 0, slot_of(-d))
-        start(low_at[d] & can_up, 0, slot_of(-d), UP)
-        start(low_at[d], 0, slot_of(-d), CC)
-        arrive(high_at[d], 0, slot_of(d))
-        start(high_at[d] & can_down, 0, slot_of(d), DOWN)
-        start(high_at[d], 0, slot_of(d), CC)
+    def gates_on(slot_of, d, from_low=None, from_high=None):
+        from_low = low_at[d] if from_low is None else from_low
+        from_high = high_at[d] if from_high is None else from_high
+        arrive(from_low, 0, slot_of(-d))
+        start(from_low & can_up, 0, slot_of(-d), UP)
+        start(from_low, 0, slot_of(-d), CC)
+        arrive(from_high, 0, slot_of(d))
+        start(from_high & can_down, 0, slot_of(d), DOWN)
+        start(from_high, 0, slot_of(d), CC)
 
     def tokens_on(d):
         for k in TOKS:
@@ -381,21 +381,20 @@
             for k, term in enumerate(split3(full)):
                 out[k, esl, :] = term
 
+    def cross_on(go_up, go_down):
+        for k in (0, 1, 2):
+            start(go_up, k, ys(0), UP, across[k])
+            start(go_down, k, ys(0), DOWN, across[k])
+
     gates_on(zs, 1)
     arrive(None, 0, ys(0))
-    start(can_up, 0, ys(0), UP)
-    start(can_down, 0, ys(0), DOWN)
+    cross_on(z < 2, z > 1)
     start(None, 0, ys(0), CC)
-    gates_on(zs, 2)
-    gates_on(ys, 1)
     products(z)
     tokens_on(2)
-    for k in TOKS:
-        start(z == 2, k, ys(0), UP, across[k])
-        start(z == 1, k, ys(0), DOWN, across[k])
-    gates_on(zs, 3)
-    gates_on(ys, 2)
-    gates_on(ys, 3)
+    gates_on(zs, 2)
+    gates_on(ys, 1, middle, middle)
+    cross_on(z == 2, z == 1)
 
     gates = jnp.concatenate([g_ref[0:32, 0:64], g_ref[0:32, 64:128], g_ref[32:64, 0:64], g_ref[32:64, 64:128]], axis=0)
     for s in range(1, 4):
@@ -410,16 +409,20 @@
         out[...] = (full[0:64] + full[64:128] + full[128:192]).astype(BF16)
 
     tokens_on(3)
+    gates_on(zs, 3)
     crossed(middle, -1)
     crossed(middle, 1)
+    gates_on(ys, 2)
     when(middle, lambda: products(z - 1))
     when(middle, lambda: products(z + 1))
     crossed(low_at[2], -2)
     crossed(high_at[2], 2)
     products(lax.rem(z + 2, 4))
+    gates_on(ys, 1, z == 3, z == 0)
     crossed(z == 3, -1)
     crossed(z == 0, 1)
     when(ends, lambda: products(1 + z // 3))
+    gates_on(ys, 3)
     crossed(low_at[3], -3)
     crossed(high_at[3], 3)
     when(ends, lambda: products(3 - z))
@@ -479,6 +482,10 @@
     over_slots(lambda k: patch(k, dv_hbm, vres, 1).wait())
 
 
+def in_hbm(*vals):
+    return [pltpu.with_memory_space_constraint(val, pltpu.HBM) for val in vals]
+
+
 def solution(mesh):
     tok_spec = P(('replica', 'data', 'table'))
     row_spec = P(('replica', 'table'))
@@ -500,7 +507,7 @@
             in_specs=[HBM] * 3, out_specs=[VMEM] * 7,
             scratch_shapes=[dma((16,)), dma((15,)), dma((2, 3)), dma((2, 3))],
             compiler_params=pltpu.CompilerParams(collective_id=0, has_side_effects=True, vmem_limit_bytes=4 * MB),
-        )(wanted, tok, dy)
+        )(*in_hbm(wanted, tok, dy))
         du, g_own, ru, rv, vslot, meta = pl.pallas_call(
             prep_kernel,
             out_shape=[table, shape((64, 128), F32), rows, rows, shape((8, 512), jnp.int32), shape((8, 512), F32)],
@@ -512,7 +519,7 @@
                 pltpu.SMEM((8, 512), jnp.int32), dma, dma((2,)), dma, dma((2,)),
             ],
             compiler_params=pltpu.CompilerParams(vmem_limit_bytes=36 * MB),
-        )(u, v, pick_t, gate_t, ids)
+        )(u, v, *in_hbm(pick_t, gate_t), ids)
         pu, pv, y, dx = pl.pallas_call(
             main_kernel,
             out_shape=[shape((3, 512, width), BF16)] * 2 + [block] * 2,

time: 73.5 us -> 59.6 us (0.81); the launches traced: 72.3 us -> 59.3 us
  Pallas kernels: 67.5 us -> 58.6 us
  local copies, waits for them, and re-layouts: 4.12 us -> 0.01 us
    pallas_call x1, Pallas kernels: 33.6 us -> 24.7 us  [device_step(): pl.pallas_call(main_kernel, out_shape=[shape((3, 512, width), BF16)] * 2...]
    unnamed x14 -> x4, local copies, waits for them, and re-layouts: 4.12 us -> 0.01 us
where the time goes in v1:
time: 59.6 us; the launch traced here: 59.3 us
  Pallas kernels  58.6 us (98%)
  between operations  0.69 us (1%)
    pallas_call x1, Pallas kernels, device_step(): pl.pallas_call(main_kernel, out_shape=[shape((3, 512, width), BF16)] * 2...  24.7 us
    pallas_call x1, Pallas kernels, device_step(): pl.pallas_call(first_kernel, out_shape=[shape((16, 1, 128), jnp.int32)] +...  12.6 us
    pallas_call x1, Pallas kernels, device_step(): pl.pallas_call(put_kernel, out_shape=[table, table, block, block], in_spe...  11.5 us
    pallas_call x1, Pallas kernels, device_step(): pl.pallas_call(prep_kernel, out_shape=[table, shape((64, 128), F32), rows...  9.81 us

profile of v1, /device:TPU:0, one launch (start us, length us, event | category | flops | bytes accessed | tf_op | source)
XLA Modules:
  0.0 59.3 jit_solution(6426024167642576669)
XLA Ops:
  0.6 12.6 %shard_map.102 = (s32[16,1,128]{2,1,0:T(1,128)S(1)}, bf16[64,768]{1,0:T(8,128)(2,1)S(1)}, bf16[64,768]{1,0:T(8,128)(2,1)S(1)}, bf16[64,768]{1,0:T(8,128)(2,1)S(1...) custom-call(s32[1,128]{1,0:T(1,128)} %ids_ref.1, bf16[64,768]{1,0:T(8,128)(2,1)} %x_ref.3, ...), custom_call_target="tpu_custom_call" | custom-call | tf_op jit(solution)/shard_map/pallas_call | solution.py:505
  13.3 0.0 copy-start
  13.3 0.0 copy-start.1
  13.3 9.8 %shard_map.103 = (bf16[16384,768]{1,0:T(8,128)(2,1)}, f32[64,128]{1,0:T(8,128)S(1)}, bf16[512,768]{1,0:T(8,128)(2,1)S(1)}, bf16[512,768]{1,0:T(8,128)(2,1)S(1)},...) custom-call(bf16[16384,768]{1,0:T(8,128)(2,1)} %u_hbm.1, bf16[16384,768]{1,0:T(8,128)(2,1)} %v_hbm.1, s32[128,64]{1,0:T(8,128)} %bitcast.6, ...), custom_call_target="tpu_custom_call" | custom-call | tf_op jit(solution)/shard_map/pallas_call | solution.py:511
  23.1 0.0 copy-done
  23.1 0.0 copy-done.1
  23.1 24.7 %shard_map.104 = (bf16[3,512,768]{2,1,0:T(8,128)(2,1)S(1)}, bf16[3,512,768]{2,1,0:T(8,128)(2,1)S(1)}, bf16[64,768]{1,0:T(8,128)(2,1)S(1)}, bf16[64,768]{1,0:T(8,128)(2,1)S(1)}) custom-call(bf16[64,768]{1,0:T(8,128)(2,1)S(1)} %copy-done, bf16[64,768]{1,0:T(8,128)(2,1)S(1)} %copy-done.1, f32[64,128]{1,0:T(8,128)S(1)} %get-tuple-element.26.g_ref, ...), custom_call_target="tpu_custom_call" | custom-call | tf_op jit(solution)/shard_map/pallas_call | solution.py:523
  47.8 11.5 %shard_map.105 = (bf16[16384,768]{1,0:T(8,128)(2,1)}, bf16[16384,768]{1,0:T(8,128)(2,1)}, bf16[64,768]{1,0:T(8,128)(2,1)}, bf16[64,768]{1,0:T(8,128)(2,1)}) custom-call(bf16[3,512,768]{2,1,0:T(8,128)(2,1)S(1)} %get-tuple-element.35.pu, bf16[3,512,768]{2,1,0:T(8,128)(2,1)S(1)} %get-tuple-element.36.pv, ...), custom_call_target="tpu_custom_call", output_to_operand_aliasing={{0}: (6, {})} | custom-call | tf_op jit(solution)/shard_map/pallas_call | solution.py:534
Async XLA Ops:
  13.3 9.8 %copy-start = (bf16[64,768]{1,0:T(8,128)(2,1)S(1)}, bf16[64,768]{1,0:T(8,128)(2,1)}, u32[]{:S(2)}) copy-start(bf16[64,768]{1,0:T(8,128)(2,1)} %x_ref.3) | copy-start | bytes 294916
  13.3 9.8 %copy-start.1 = (bf16[64,768]{1,0:T(8,128)(2,1)S(1)}, bf16[64,768]{1,0:T(8,128)(2,1)}, u32[]{:S(2)}) copy-start(bf16[64,768]{1,0:T(8,128)(2,1)} %dy_ref.3) | copy-start | bytes 294916

commit v2 on v1

--- a/solution.py
+++ b/solution.py
@@ -18,6 +18,10 @@
 SMEM = pl.BlockSpec(memory_space=pltpu.SMEM)
 MB = 1024 * 1024
 UP, DOWN, YY, CC = range(4)
+EARLY = 2048
+OTHERS = (2, 1, 3)
+ALL3 = (0, 1, 2)
+PAIR = (0, 1)
 
 
 def gelu_pair(pre_act):
@@ -40,7 +44,21 @@
     return lax.dot_general(a, b, dims, preferred_element_type=F32)
 
 
-def first_kernel(ids_ref, x_ref, dy_ref, ids_out, xd, dyd, xu, dyu, xy, dyy, ssem, rsem, hops, hopr):
+def thirds(val):
+    one, two, three = jnp.split(val, 3, axis=0)
+    return one + two + three
+
+
+def seg(i, n):
+    return pl.ds(pl.multiple_of(i * n, n), n)
+
+
+def iota(shape, axis):
+    return lax.broadcasted_iota(jnp.int32, shape, axis)
+
+
+def first_kernel(ids_ref, x_hbm, dy_hbm, pick_hbm, gate_hbm, ids_out, g_out, xd, dyd, xu, dyu, xy, dyy,
+                 x_ref, dy_ref, pick_ref, gate_ref, lsem, ssem, rsem, hops, hopr):
     z = lax.axis_index("data")
     t = lax.axis_index("table")
     me = z * 4 + t
@@ -48,6 +66,32 @@
     peers = [(lax.rem(z + dz, 4), lax.rem(t + dt, 4)) for dz in range(4) for dt in range(4)][1:]
     for pz, pt in peers:
         pl.semaphore_signal(bar, inc=1, device_id={"data": pz, "table": pt}, device_id_type=MESH)
+    loads = [
+        pltpu.make_async_copy(src, dst, lsem.at[i])
+        for i, (src, dst) in enumerate(((pick_hbm, pick_ref), (gate_hbm, gate_ref), (x_hbm, x_ref), (dy_hbm, dy_ref)))
+    ]
+    for one in loads:
+        one.start()
+    loads[0].wait()
+    loads[1].wait()
+
+    sel, tok = pick_ref.shape
+    quarter = sel // 4
+    row = iota((2 * quarter, 2 * tok), 0)
+    row = row + jnp.where(row >= quarter, quarter, 0)
+
+    def add_gates(i, acc):
+        pick8 = pick_ref[seg(i, 8), :]
+        gate8 = gate_ref[seg(i, 8), :]
+        pick8 = jnp.concatenate([pick8, pick8 - quarter], axis=1)
+        gate8 = jnp.concatenate([gate8, gate8], axis=1)
+        for j in range(8):
+            acc = acc + jnp.where(row == pick8[j : j + 1, :], gate8[j : j + 1, :], 0.0)
+        return acc
+
+    g_out[...] = lax.fori_loop(0, sel // 8, add_gates, jnp.zeros((2 * quarter, 2 * tok), F32))
+    loads[2].wait()
+    loads[3].wait()
     pl.semaphore_wait(bar, 15)
     copies = []
     for i, (pz, pt) in enumerate(peers):
@@ -65,7 +109,7 @@
             device_id=peer, device_id_type=MESH,
         )
 
-    for k in range(2):
+    for k in PAIR:
         hop(k, 2).start()
 
         @pl.when(z < 3)
@@ -81,7 +125,7 @@
     local.wait()
     for one in copies:
         one.wait()
-    for k in range(2):
+    for k in PAIR:
         hop(k, 2).wait()
 
         @pl.when(z < 3)
@@ -95,16 +139,12 @@
             hop(k, 0).wait_recv()
 
 
-def prep_kernel(u_hbm, v_hbm, pick_hbm, gate_hbm, ids_ref, du_hbm, g_out, rows_u, rows_v, vslot, meta,
-                zbuf, ugrp, vgrp, uacc, vacc, pick_ref, gate_ref, sslot, zsem, gsem, ssem, isem):
+def prep_kernel(u_hbm, v_hbm, ids_ref, du_hbm, dv_hbm, rows_u, rows_v, vslot, meta,
+                zbuf, ugrp, vgrp, uacc, vacc, sslot, zsem, gsem, ssem):
     r = lax.axis_index("table")
     n_local = u_hbm.shape[0]
     n_ent = rows_u.shape[0]
     zrows = zbuf.shape[0]
-    load_pick = pltpu.make_async_copy(pick_hbm, pick_ref, isem.at[0])
-    load_gate = pltpu.make_async_copy(gate_hbm, gate_ref, isem.at[1])
-    load_pick.start()
-    load_gate.start()
     zbuf[...] = jnp.zeros_like(zbuf)
 
     ids = jnp.concatenate([ids_ref[e] for e in range(16)], axis=0).astype(F32)
@@ -113,14 +153,13 @@
         pick = jnp.where(r == o, ids[:, o * 32 : o * 32 + 32], pick)
     pick = pick - (r * n_local).astype(F32)
     idrow = jnp.concatenate([pick[e : e + 1, :] for e in range(16)], axis=1)
-    ii = lax.broadcasted_iota(jnp.int32, (n_ent, n_ent), 0)
-    jj = lax.broadcasted_iota(jnp.int32, (n_ent, n_ent), 1)
-
-    def fill(i):
-        return pltpu.make_async_copy(zbuf, du_hbm.at[pl.ds(i * zrows, zrows), :], zsem)
-
-    for i in range(n_local // zrows):
-        fill(i).start()
+    ii = iota((n_ent, n_ent), 0)
+    jj = iota((n_ent, n_ent), 1)
+
+    fills = [pltpu.make_async_copy(zbuf, du_hbm.at[pl.ds(i, zrows), :], zsem) for i in range(0, n_local, zrows)]
+    fills += [pltpu.make_async_copy(zbuf, dv_hbm.at[pl.ds(i, zrows), :], zsem) for i in range(0, EARLY, zrows)]
+    for one in fills:
+        one.start()
 
     def lanes(cond, val):
         return jnp.sum(jnp.where(cond, val, 0.0), axis=1, keepdims=True)
@@ -153,8 +192,8 @@
     n_blk = (sslot[1, 0] + 31) // 32
 
     def fetch(k, table, grp, s):
-        g = pl.multiple_of(sslot[0, k] * 8, 8)
-        return pltpu.make_async_copy(table.at[pl.ds(g, 8), :], grp.at[pl.ds(pl.multiple_of(k * 8, 8), 8), :], gsem.at[s])
+        g = seg(sslot[0, k], 8)
+        return pltpu.make_async_copy(table.at[g, :], grp.at[seg(k, 8), :], gsem.at[s])
 
     def start_fetch(k, carry):
         fetch(k, u_hbm, ugrp, 0).start()
@@ -167,47 +206,27 @@
         return carry
 
     lax.fori_loop(0, n_blk * 32, start_fetch, 0)
-
-    load_pick.wait()
-    load_gate.wait()
-    sel, tok = pick_ref.shape
-    quarter = sel // 4
-    row = lax.broadcasted_iota(jnp.int32, (2 * quarter, 2 * tok), 0)
-    row = row + jnp.where(row >= quarter, quarter, 0)
-
-    def add_gates(i, acc):
-        base = pl.multiple_of(i * 8, 8)
-        pick8 = pick_ref[pl.ds(base, 8), :]
-        gate8 = gate_ref[pl.ds(base, 8), :]
-        pick8 = jnp.concatenate([pick8, pick8 - quarter], axis=1)
-        gate8 = jnp.concatenate([gate8, gate8], axis=1)
-        for j in range(8):
-            acc = acc + jnp.where(row == pick8[j : j + 1, :], gate8[j : j + 1, :], 0.0)
-        return acc
-
-    g_out[...] = lax.fori_loop(0, sel // 8, add_gates, jnp.zeros((2 * quarter, 2 * tok), F32))
-
     lax.fori_loop(0, n_blk * 32, wait_fetch, 0)
 
     uacc[...] = jnp.zeros_like(uacc)
     vacc[...] = jnp.zeros_like(vacc)
-    kk = lax.broadcasted_iota(jnp.int32, (n_ent, 256), 0)
-    qk = lax.broadcasted_iota(jnp.int32, (n_ent, 256), 1) >> 3
-    q7 = (lax.broadcasted_iota(jnp.int32, (1, 256), 1) & 7).astype(F32)
+    kk = iota((n_ent, 256), 0)
+    qk = iota((n_ent, 256), 1) >> 3
+    q7 = (iota((1, 256), 1) & 7).astype(F32)
 
     def take_rows(b, carry):
         rowid = 8.0 * subl(kk == qk + b * 32, jnp.broadcast_to(slot_col, (n_ent, 256))) + q7
         pickm = jnp.where(idcol == rowid, 1.0, 0.0).astype(BF16)
-        base = pl.multiple_of(b * 256, 256)
-        uacc[...] += dot(pickm, ugrp[pl.ds(base, 256), :])
-        vacc[...] += dot(pickm, vgrp[pl.ds(base, 256), :])
+        base = seg(b, 256)
+        uacc[...] += dot(pickm, ugrp[base, :])
+        vacc[...] += dot(pickm, vgrp[base, :])
         return carry
 
     lax.fori_loop(0, n_blk, take_rows, 0)
     rows_u[...] = uacc[...].astype(BF16)
     rows_v[...] = vacc[...].astype(BF16)
-    for i in range(n_local // zrows):
-        fill(i).wait()
+    for one in fills:
+        one.wait()
 
 
 def main_kernel(x_ref, dy_ref, g_ref, xd, dyd, xu, dyu, xy, dyy, ru, rv, pu, pv, y_out, dx_out,
@@ -222,8 +241,8 @@
     up, down = {"data": z + 1}, {"data": z - 1}
     peers = {UP: up, DOWN: down, YY: y_peer, CC: c_peer}
     tok = x_ref.shape[0]
-    low_at = {d: z - d >= 0 for d in (1, 2, 3)}
-    high_at = {d: z + d <= 3 for d in (1, 2, 3)}
+    low_at = {d: z - d >= 0 for d in OTHERS}
+    high_at = {d: z + d <= 3 for d in OTHERS}
     can_up, can_down = high_at[1], low_at[1]
     middle = can_up & can_down
     ends = (z == 0) | (z == 3)
@@ -249,7 +268,7 @@
     def place(k, slot):
         if k == 0:
             return gx.at[slot]
-        return outs[k].at[pl.ds(pl.multiple_of(slot * tok, tok), tok), :]
+        return outs[k].at[seg(slot, tok), :]
 
     def copy(k, slot, lane, src=None):
         ref = place(k, slot)
@@ -283,8 +302,8 @@
     def send_row(k, s):
         to = lax.rem(t + s, 4)
         return pltpu.make_async_remote_copy(
-            src_ref=(ru, rv)[k].at[pl.ds(pl.multiple_of(z * 128 + to * 32, 32), 32), :],
-            dst_ref=(ubuf, vbuf)[k].at[pl.ds(pl.multiple_of(t * 32, 32), 32), :],
+            src_ref=(ru, rv)[k].at[seg(z * 4 + to, 32), :],
+            dst_ref=(ubuf, vbuf)[k].at[seg(t, 32), :],
             send_sem=rows_s.at[k, s], recv_sem=rows_r.at[k, s],
             device_id={"table": to}, device_id_type=MESH,
         )
@@ -294,8 +313,8 @@
     high = (None, xu, dyu)
     across = (None, xy, dyy)
     me = zs(0)
-    my_half = g_ref.at[pl.ds(pl.multiple_of(y * 32, 32), 32), :]
-    other_half = g_ref.at[pl.ds(pl.multiple_of((1 - y) * 32, 32), 32), :]
+    my_half = g_ref.at[seg(y, 32), :]
+    other_half = g_ref.at[seg(1 - y, 32), :]
 
     start(can_up, 0, me, UP, my_half)
     start(can_down, 0, me, DOWN, my_half)
@@ -304,8 +323,8 @@
     for k in TOKS:
         start(middle, k, zs(-1), UP, low[k])
         start(middle, k, zs(1), DOWN, high[k])
-    for k in range(2):
-        for s in (2, 1, 3):
+    for k in PAIR:
+        for s in OTHERS:
             send_row(k, s).start()
     for k in TOKS:
         start(None, k, me, CC, own[k])
@@ -315,19 +334,19 @@
 
     def keep(cond, k, slot, src):
         def run():
-            outs[k][pl.ds(pl.multiple_of(slot * tok, tok), tok), :] = src[...]
+            outs[k][seg(slot, tok), :] = src[...]
 
         when(cond, run)
 
-    gx[me] = g_ref[pl.ds(pl.multiple_of(y * 32, 32), 32), :]
+    gx[me] = g_ref[seg(y, 32), :]
     for k in TOKS:
         keep(None, k, me, own[k])
         keep(None, k, ys(0), across[k])
         keep(can_down, k, zs(-1), low[k])
         keep(can_up, k, zs(1), high[k])
-    mine = pl.ds(pl.multiple_of(t * 32, 32), 32)
-    ubuf[mine, :] = ru[pl.ds(pl.multiple_of(z * 128 + t * 32, 32), 32), :]
-    vbuf[mine, :] = rv[pl.ds(pl.multiple_of(z * 128 + t * 32, 32), 32), :]
+    mine = seg(t, 32)
+    ubuf[mine, :] = ru[seg(z * 4 + t, 32), :]
+    vbuf[mine, :] = rv[seg(z * 4 + t, 32), :]
 
     def gates_on(slot_of, d, from_low=None, from_high=None):
         from_low = low_at[d] if from_low is None else from_low
@@ -355,14 +374,14 @@
             arrive(cond, k, ys(d))
             start(cond, k, ys(d), CC)
 
-    diag = (lax.broadcasted_iota(jnp.int32, (128, 256), 0) >> 5) == (lax.broadcasted_iota(jnp.int32, (128, 256), 1) >> 6)
+    diag = (iota((128, 256), 0) >> 5) == (iota((128, 256), 1) >> 6)
 
     def products(d):
         for tt in (t_c, t_yc):
-            for k in range(3):
+            for k in ALL3:
                 arrive(None, k, d * 4 + tt)
-        tsl = pl.ds(pl.multiple_of(d * 256, 256), 256)
-        esl = pl.ds(pl.multiple_of(d * 128, 128), 128)
+        tsl = seg(d, 256)
+        esl = seg(d, 128)
         x4, dy4 = tx[tsl, :], ty[tsl, :]
         u4, v4 = ru[esl, :], rv[esl, :]
         gates = []
@@ -377,12 +396,12 @@
         c4 = jnp.where(diag, g4 * slope * b4, 0.0)
         for coef, val, out in ((c4, x4, pu), (w4, dy4, pv)):
             full = dot(jnp.concatenate(split3(coef), axis=0), val)
-            full = full[0:128] + full[128:256] + full[256:384]
+            full = thirds(full)
             for k, term in enumerate(split3(full)):
                 out[k, esl, :] = term
 
     def cross_on(go_up, go_down):
-        for k in (0, 1, 2):
+        for k in ALL3:
             start(go_up, k, ys(0), UP, across[k])
             start(go_down, k, ys(0), DOWN, across[k])
 
@@ -397,7 +416,7 @@
     cross_on(z == 2, z == 1)
 
     gates = jnp.concatenate([g_ref[0:32, 0:64], g_ref[0:32, 64:128], g_ref[32:64, 0:64], g_ref[32:64, 64:128]], axis=0)
-    for s in range(1, 4):
+    for s in OTHERS:
         send_row(0, s).wait_recv()
         send_row(1, s).wait_recv()
     act, slope = gelu_pair(dot(ubuf[...], x_ref[...], NT))
@@ -406,7 +425,7 @@
     c_val = jnp.transpose(gates * slope * b_val)
     for coef, rows, out in ((w_val, vbuf, y_out), (c_val, ubuf, dx_out)):
         full = dot(jnp.concatenate(split3(coef), axis=0), rows[...])
-        out[...] = (full[0:64] + full[64:128] + full[128:192]).astype(BF16)
+        out[...] = (thirds(full)).astype(BF16)
 
     tokens_on(3)
     gates_on(zs, 3)
@@ -421,20 +440,21 @@
     gates_on(ys, 1, z == 3, z == 0)
     crossed(z == 3, -1)
     crossed(z == 0, 1)
-    when(ends, lambda: products(1 + z // 3))
-    gates_on(ys, 3)
     crossed(low_at[3], -3)
     crossed(high_at[3], 3)
+    gates_on(ys, 3)
+    when(ends, lambda: products(1 + z // 3))
     when(ends, lambda: products(3 - z))
 
-    for k in range(2):
-        for s in range(1, 4):
+    for k in PAIR:
+        for s in OTHERS:
             send_row(k, s).wait_send()
     for cond, k, slot, lane in sent:
         when(cond, lambda k=k, slot=slot, lane=lane: copy(k, slot, lane).wait_send())
 
 
-def put_kernel(pu, pv, y_ref, dx_ref, sslot, meta, du_in, du_hbm, dv_hbm, y_out, dx_out, zbuf, ures, vres, zsem, psem):
+def put_kernel(pu, pv, y_ref, dx_ref, sslot, meta, du_in, dv_in, du_hbm, dv_hbm, y_out, dx_out,
+               zbuf, ures, vres, zsem, psem):
     n_ent = pu.shape[1]
     zrows = zbuf.shape[0]
     zbuf[...] = jnp.zeros_like(zbuf)
@@ -443,43 +463,39 @@
     n_slot = sslot[1, 0]
     n_blk = (n_slot + 31) // 32
     idrow, slot_row = meta[0:1, :], meta[1:2, :]
-    kq = lax.broadcasted_iota(jnp.int32, (256, n_ent), 1)
-    qq = lax.broadcasted_iota(jnp.int32, (256, n_ent), 0) >> 3
-    q7 = (lax.broadcasted_iota(jnp.int32, (256, 1), 0) & 7).astype(F32)
-
-    def fill(i):
-        return pltpu.make_async_copy(zbuf, dv_hbm.at[pl.ds(i * zrows, zrows), :], zsem)
-
-    for i in range(dv_hbm.shape[0] // zrows):
-        fill(i).start()
+    fills = [pltpu.make_async_copy(zbuf, dv_hbm.at[pl.ds(i, zrows), :], zsem) for i in range(EARLY, dv_hbm.shape[0], zrows)]
+    for one in fills:
+        one.start()
+    kq = iota((256, n_ent), 1)
+    qq = iota((256, n_ent), 0) >> 3
+    q7 = (iota((256, 1), 0) & 7).astype(F32)
 
     def patch(k, table, res, s):
-        g = pl.multiple_of(sslot[0, k] * 8, 8)
-        return pltpu.make_async_copy(res.at[pl.ds(pl.multiple_of(k * 8, 8), 8), :], table.at[pl.ds(g, 8), :], psem.at[s])
+        g = seg(sslot[0, k], 8)
+        return pltpu.make_async_copy(res.at[seg(k, 8), :], table.at[g, :], psem.at[s])
+
+    def over_slots(lo, hi, run):
+        def body(k, carry):
+            run(k)
+            return carry
+
+        lax.fori_loop(lo, hi, body, 0)
 
     def put_rows(b, carry):
         rowid = 8.0 * jnp.sum(jnp.where(kq == qq + b * 32, slot_row, 0.0), axis=1, keepdims=True) + q7
         spread = jnp.where(rowid == idrow, 1.0, 0.0).astype(BF16)
-        base = pl.multiple_of(b * 256, 256)
-        ures[pl.ds(base, 256), :] = (dot(spread, pu[0]) + dot(spread, pu[1]) + dot(spread, pu[2])).astype(BF16)
-        vres[pl.ds(base, 256), :] = (dot(spread, pv[0]) + dot(spread, pv[1]) + dot(spread, pv[2])).astype(BF16)
+        base = seg(b, 256)
+        ures[base, :] = (dot(spread, pu[0]) + dot(spread, pu[1]) + dot(spread, pu[2])).astype(BF16)
+        vres[base, :] = (dot(spread, pv[0]) + dot(spread, pv[1]) + dot(spread, pv[2])).astype(BF16)
+        over_slots(b * 32, jnp.minimum(b * 32 + 32, n_slot), lambda k: patch(k, du_hbm, ures, 0).start())
         return carry
 
     lax.fori_loop(0, n_blk, put_rows, 0)
-
-    def over_slots(run):
-        def body(k, carry):
-            run(k)
-            return carry
-
-        lax.fori_loop(0, n_slot, body, 0)
-
-    over_slots(lambda k: patch(k, du_hbm, ures, 0).start())
-    for i in range(dv_hbm.shape[0] // zrows):
-        fill(i).wait()
-    over_slots(lambda k: patch(k, dv_hbm, vres, 1).start())
-    over_slots(lambda k: patch(k, du_hbm, ures, 0).wait())
-    over_slots(lambda k: patch(k, dv_hbm, vres, 1).wait())
+    for one in fills:
+        one.wait()
+    over_slots(0, n_slot, lambda k: patch(k, dv_hbm, vres, 1).start())
+    over_slots(0, n_slot, lambda k: patch(k, du_hbm, ures, 0).wait())
+    over_slots(0, n_slot, lambda k: patch(k, dv_hbm, vres, 1).wait())
 
 
 def in_hbm(*vals):
@@ -502,24 +518,28 @@
         pick_t = jnp.transpose(pick, (1, 2, 0)).reshape(sel, n_tok)
         gate_t = jnp.transpose(gate, (1, 2, 0)).reshape(sel, n_tok)
 
-        ids, *hops = pl.pallas_call(
-            first_kernel, out_shape=[shape((16, 1, 128), jnp.int32)] + [block] * 6,
-            in_specs=[HBM] * 3, out_specs=[VMEM] * 7,
-            scratch_shapes=[dma((16,)), dma((15,)), dma((2, 3)), dma((2, 3))],
+        ids, g_own, *hops = pl.pallas_call(
+            first_kernel,
+            out_shape=[shape((16, 1, 128), jnp.int32), shape((64, 128), F32)] + [block] * 6,
+            in_specs=[HBM] * 5, out_specs=[VMEM] * 8,
+            scratch_shapes=[
+                pltpu.VMEM((n_tok, width), BF16), pltpu.VMEM((n_tok, width), BF16),
+                pltpu.VMEM((sel, n_tok), jnp.int32), pltpu.VMEM((sel, n_tok), F32),
+                dma((4,)), dma((16,)), dma((15,)), dma((2, 3)), dma((2, 3)),
+            ],
             compiler_params=pltpu.CompilerParams(collective_id=0, has_side_effects=True, vmem_limit_bytes=4 * MB),
-        )(*in_hbm(wanted, tok, dy))
-        du, g_own, ru, rv, vslot, meta = pl.pallas_call(
+        )(*in_hbm(wanted, tok, dy, pick_t, gate_t))
+        du, dv, ru, rv, vslot, meta = pl.pallas_call(
             prep_kernel,
-            out_shape=[table, shape((64, 128), F32), rows, rows, shape((8, 512), jnp.int32), shape((8, 512), F32)],
-            in_specs=[HBM] * 4 + [VMEM], out_specs=[HBM] + [VMEM] * 5,
+            out_shape=[table, table, rows, rows, shape((8, 512), jnp.int32), shape((8, 512), F32)],
+            in_specs=[HBM] * 2 + [VMEM], out_specs=[HBM] * 2 + [VMEM] * 4,
             scratch_shapes=[
                 pltpu.VMEM((512, width), BF16), pltpu.VMEM((4096, width), BF16), pltpu.VMEM((4096, width), BF16),
                 pltpu.VMEM((512, width), F32), pltpu.VMEM((512, width), F32),
-                pltpu.VMEM((sel, n_tok), jnp.int32), pltpu.VMEM((sel, n_tok), F32),
-                pltpu.SMEM((8, 512), jnp.int32), dma, dma((2,)), dma, dma((2,)),
+                pltpu.SMEM((8, 512), jnp.int32), dma, dma((2,)), dma,
             ],
             compiler_params=pltpu.CompilerParams(vmem_limit_bytes=36 * MB),
-        )(u, v, *in_hbm(pick_t, gate_t), ids)
+        )(u, v, ids)
         pu, pv, y, dx = pl.pallas_call(
             main_kernel,
             out_shape=[shape((3, 512, width), BF16)] * 2 + [block] * 2,
@@ -527,21 +547,21 @@
             scratch_shapes=[
                 pltpu.VMEM((16 * n_tok, width), BF16), pltpu.VMEM((16 * n_tok, width), BF16),
                 pltpu.VMEM((16, 32, 128), F32), pltpu.VMEM((128, width), BF16), pltpu.VMEM((128, width), BF16),
-                dma((3, 4, 16)), dma((3, 16)), dma((2, 4)), dma((2, 4)),
+                dma((3, 4, 16)), dma((3, 16)), *[dma((2, 4))] * 2,
             ],
             compiler_params=pltpu.CompilerParams(collective_id=1, has_side_effects=True, vmem_limit_bytes=32 * MB),
         )(tok, dy, g_own, *hops, ru, rv)
         du, dv, y, dx = pl.pallas_call(
             put_kernel,
             out_shape=[table, table, block, block],
-            in_specs=[VMEM] * 4 + [SMEM, VMEM, HBM], out_specs=[HBM, HBM, VMEM, VMEM],
+            in_specs=[VMEM] * 4 + [SMEM, VMEM, HBM, HBM], out_specs=[HBM, HBM, VMEM, VMEM],
             scratch_shapes=[
                 pltpu.VMEM((512, width), BF16), pltpu.VMEM((4096, width), BF16), pltpu.VMEM((4096, width), BF16),
                 dma, dma((2,)),
             ],
-            input_output_aliases={6: 0},
+            input_output_aliases={6: 0, 7: 1},
             compiler_params=pltpu.CompilerParams(vmem_limit_bytes=36 * MB),
-        )(pu, pv, y, dx, vslot, meta, du)
+        )(pu, pv, y, dx, vslot, meta, du, dv)
         return y, dx, du, dv
 
     return jax.shard_map(device_step, mesh=mesh, in_specs=(tok_spec, tok_spec, row_spec, row_spec, tok_spec, tok_spec, tok_spec), out_specs=(tok_spec, tok_spec, row_spec, row_spec), check_vma=False)

time: 59.6 us -> 58.2 us (0.977); the launches traced: 59.3 us -> 57.1 us
  Pallas kernels: 58.6 us -> 56.4 us
    pallas_call x1, Pallas kernels: 24.7 us -> 22.5 us  [device_step(): pl.pallas_call(main_kernel, out_shape=[shape((3, 512, width), BF16)] * 2...]
    pallas_call x1, Pallas kernels: 11.5 us -> 10.4 us  [device_step(): pl.pallas_call(put_kernel, out_shape=[table, table, block, block], in_spe...]
    pallas_call x2, Pallas kernels: 22.4 us -> 23.5 us  [the longest x1 12.7 us: device_step(): pl.pallas_call(first_kernel, out_shape=[shape((16, 1, 128), jnp.int32), s...]
where the time goes in v2:
time: 58.2 us; the launch traced here: 57.1 us
  Pallas kernels  56.4 us (97%)
  between operations  0.69 us (1%)
    pallas_call x1, Pallas kernels, device_step(): pl.pallas_call(main_kernel, out_shape=[shape((3, 512, width), BF16)] * 2...  22.5 us
    pallas_call x1, Pallas kernels, device_step(): pl.pallas_call(first_kernel, out_shape=[shape((16, 1, 128), jnp.int32), s...  12.7 us
    pallas_call x1, Pallas kernels, device_step(): pl.pallas_call(prep_kernel, out_shape=[table, table, rows, rows, shape((8...  10.8 us
    pallas_call x1, Pallas kernels, device_step(): pl.pallas_call(put_kernel, out_shape=[table, table, block, block], in_spe...  10.4 us

profile of v2, /device:TPU:0, one launch (start us, length us, event | category | flops | bytes accessed | tf_op | source)
XLA Modules:
  0.0 57.1 jit_solution(5497743142938770240)
XLA Ops:
  0.6 12.7 %shard_map.102 = (s32[16,1,128]{2,1,0:T(1,128)S(1)}, f32[64,128]{1,0:T(8,128)S(1)}, bf16[64,768]{1,0:T(8,128)(2,1)S(1)}, bf16[64,768]{1,0:T(8,128)(2,1)S(1)}, bf...) custom-call(s32[1,128]{1,0:T(1,128)} %ids_ref.1, ...), custom_call_target="tpu_custom_call" | custom-call | tf_op jit(solution)/shard_map/pallas_call | solution.py:521
  13.3 0.0 copy-start
  13.4 0.0 copy-start.1
  13.4 10.8 %shard_map.103 = (bf16[16384,768]{1,0:T(8,128)(2,1)}, bf16[16384,768]{1,0:T(8,128)(2,1)}, bf16[512,768]{1,0:T(8,128)(2,1)S(1)}, bf16[512,768]{1,0:T(8,128)(2,1)S...) custom-call(bf16[16384,768]{1,0:T(8,128)(2,1)} %u_hbm.1, bf16[16384,768]{1,0:T(8,128)(2,1)} %v_hbm.1, ...), custom_call_target="tpu_custom_call" | custom-call | tf_op jit(solution)/shard_map/pallas_call | solution.py:532
  24.1 0.0 copy-done
  24.1 0.0 copy-done.1
  24.1 22.5 %shard_map.104 = (bf16[3,512,768]{2,1,0:T(8,128)(2,1)S(1)}, bf16[3,512,768]{2,1,0:T(8,128)(2,1)S(1)}, bf16[64,768]{1,0:T(8,128)(2,1)S(1)}, bf16[64,768]{1,0:T(8,128)(2,1)S(1)}) custom-call(bf16[64,768]{1,0:T(8,128)(2,1)S(1)} %copy-done, bf16[64,768]{1,0:T(8,128)(2,1)S(1)} %copy-done.1, f32[64,128]{1,0:T(8,128)S(1)} %get-tuple-element.26.g_ref, ...), custom_call_target="tpu_custom_call" | custom-call | tf_op jit(solution)/shard_map/pallas_call | solution.py:543
  46.7 10.4 %shard_map.105 = (bf16[16384,768]{1,0:T(8,128)(2,1)}, bf16[16384,768]{1,0:T(8,128)(2,1)}, bf16[64,768]{1,0:T(8,128)(2,1)}, bf16[64,768]{1,0:T(8,128)(2,1)}) custom-call(bf16[3,512,768]{2,1,0:T(8,128)(2,1)S(1)} %get-tuple-element.36.pu, bf16[3,512,768]{2,1,0:T(8,128)(2,1)S(1)} %get-tuple-element.37.pv, ...), custom_call_target="tpu_custom_call", output_to_operand_aliasing={{0}: (6, {}), {1}: (7, {})} | custom-call | tf_op jit(solution)/shard_map/pallas_call | solution.py:554
Async XLA Ops:
  13.3 10.8 %copy-start = (bf16[64,768]{1,0:T(8,128)(2,1)S(1)}, bf16[64,768]{1,0:T(8,128)(2,1)}, u32[]{:S(2)}) copy-start(bf16[64,768]{1,0:T(8,128)(2,1)} %x_ref.1) | copy-start | bytes 294916
  13.4 10.8 %copy-start.1 = (bf16[64,768]{1,0:T(8,128)(2,1)S(1)}, bf16[64,768]{1,0:T(8,128)(2,1)}, u32[]{:S(2)}) copy-start(bf16[64,768]{1,0:T(8,128)(2,1)} %dy_ref.1) | copy-start | bytes 294916
